TPU v7x, 512 devices: a whole 4x8x8 slice. The times are simulated.
512 devices in a mesh: heads: 16 (over y, core), batch: 32 (over z, x).
Axes of the slice: x: 4, y: 8, z: 8, core: 2. Of those that a mesh axis runs over, the one named last changes fastest.
Arguments:
- queries: bfloat16 [256, 4096], P('batch', 'heads'), may hold values from -6 to 6
- keys_new: bfloat16 [256, 4096], P('batch', 'heads'), may hold values from -6 to 6
- values_new: bfloat16 [256, 4096], P('batch', 'heads'), may hold values from -6 to 6
- out_gate: bfloat16 [256, 4096], P('batch', 'heads'), may hold values from -6 to 6
- decay_logit: float32 [256, 32], P('batch', 'heads'), may hold values from -6 to 6
- beta_logit: float32 [256, 32], P('batch', 'heads'), may hold values from -6 to 6
- decay_rate: float32 [32], P('heads'), may hold values from 0.05 to 2
- state: float32 [256, 32, 128, 128], P('batch', 'heads'), may hold values from -0.6 to 0.6
- norm_gain: float32 [128], replicated, may hold values from 0.1 to 1.9
- out_proj: bfloat16 [4096, 4096], P('heads'), may hold values from -0.09375 to 0.09375
- residual: bfloat16 [256, 4096], P('batch'), may hold values from -40 to 40, as said below
- final_gain: float32 [4096], replicated, may hold values from 0.1 to 1.9
- value_weight: float32 [4096], replicated, may hold values from -0.09375 to 0.09375
- lm_head: bfloat16 [4096, 65536], P(None, ('heads', 'batch')), may hold values from -15 to 15
- sampled: int32 [256], replicated, may hold values from 0 to 65535
Outputs:
- logprob: float32 [256], P('batch')
- value: float32 [256], P('batch')
Inputs may be any that keep to these rules, and one draw needn't show every extreme that they name: The residual stream's entries have scales that differ by row and by column (up to tenfold each), so neither rows nor columns share one magnitude.
All inputs are finite; a program needn't handle non-finite values.
Results may differ from a plain program's by a relative error of at most 0.0013.
Values may be sent and summed in bfloat16 or wider, within the bound.
No kernel may reach another device: no remote copies, remote signals or barrier semaphores. Data moves between devices by JAX's collectives and lax.ppermute only.
A program may use at most 64 MiB of HBM per device.

v0:
```python
import functools

import jax
import jax.numpy as jnp
from jax import lax
from jax.experimental import pallas as pl
from jax.experimental.pallas import tpu as pltpu
from jax.sharding import Mesh
from jax.sharding import PartitionSpec as P


HEADS = ("heads_0", "heads_1")
BATCH = ("z", "x_side", "x_pair")
GROUP = ("x_pair", "z")
NEAR = ("z", "heads_0")
HEADS_BATCH = ("heads_0", "heads_1", "z", "x_side", "x_pair")
SWAP = [(0, 1), (1, 0)]


epsilon = 1e-06


def exchange(parts, axis):
    return lax.all_to_all(parts, axis, split_axis=0, concat_axis=0, tiled=True)


def any_spec():
    return pl.BlockSpec(memory_space=pltpu.HBM)


def room(mebibytes):
    return pltpu.CompilerParams(vmem_limit_bytes=mebibytes * 2**20)


def vmem_spec():
    return pl.BlockSpec(memory_space=pltpu.VMEM)


def smem_spec():
    return pl.BlockSpec(memory_space=pltpu.SMEM)


def as_column(line):
    size = line.shape[1]
    shape = (size, size)
    here = lax.broadcasted_iota(jnp.int32, shape, 0) == lax.broadcasted_iota(jnp.int32, shape, 1)
    return jnp.sum(jnp.where(here, jnp.broadcast_to(line, shape), 0.0), axis=1, keepdims=True)


def heads_kernel(*refs):
    small = 9
    inputs, out_ref, local = refs[:11], refs[11], refs[12:23]
    done_ref, sems, out_sems = refs[23:]
    q_ref, k_ref, v_ref, g_ref, dl_ref, bl_ref, gain_ref, rate_ref, res_ref = local[:small]
    state_ref, proj_ref = local[small:]
    copies = [pltpu.make_async_copy(inputs[n], local[n], sems.at[n]) for n in range(small)]
    heads = state_ref.shape[1]
    for h in range(heads):
        copies.append(
            pltpu.make_async_copy(
                inputs[small].at[:, h], state_ref.at[:, h], sems.at[small + h]
            )
        )
    blocks = 4
    wide = proj_ref.shape[1] // blocks
    for n in range(blocks):
        part = pl.ds(n * wide, wide)
        copies.append(
            pltpu.make_async_copy(
                inputs[small + 1].at[:, part], proj_ref.at[:, part], sems.at[small + heads + n]
            )
        )
    for copy in copies:
        copy.start()
    for copy in copies[:small]:
        copy.wait()
    rows = q_ref.shape[0]
    size = state_ref.shape[2]
    gain = gain_ref[...]
    queries, keys = [], []
    for h in range(heads):
        lanes = slice(h * size, (h + 1) * size)
        query = q_ref[:, lanes].astype(jnp.float32)
        key = k_ref[:, lanes].astype(jnp.float32)
        query = query / jnp.sqrt(jnp.sum(query * query, axis=1, keepdims=True) + epsilon)
        queries.append(query * size ** (-0.5))
        keys.append(key / jnp.sqrt(jnp.sum(key * key, axis=1, keepdims=True) + epsilon))
    turned = jnp.concatenate(queries + keys, axis=0).T
    parts = []
    for h in range(heads):
        lanes = slice(h * size, (h + 1) * size)
        logit = dl_ref[h : h + 1, :]
        soft = jnp.maximum(logit, 0.0) + jnp.log1p(jnp.exp(-jnp.abs(logit)))
        decay = as_column(jnp.exp(-rate_ref[:, h : h + 1] * soft))
        strength = as_column(1.0 / (1.0 + jnp.exp(-bl_ref[h : h + 1, :])))
        inter = jnp.sum(queries[h] * keys[h], axis=1, keepdims=True)
        value = v_ref[:, lanes].astype(jnp.float32)
        gate = g_ref[:, lanes].astype(jnp.float32)
        copies[small + h].wait()
        by_query, by_key = [], []
        for b in range(rows):
            block = state_ref[b, h]
            at = h * rows + b
            by_query.append(jnp.sum(turned[:, at : at + 1] * block, axis=0, keepdims=True))
            at += heads * rows
            by_key.append(jnp.sum(turned[:, at : at + 1] * block, axis=0, keepdims=True))
        state_query = jnp.concatenate(by_query, axis=0)
        state_key = jnp.concatenate(by_key, axis=0)
        written = value - decay * state_key
        output = decay * state_query + strength * inter * written
        mean = jnp.mean(output * output, axis=1, keepdims=True)
        normed = output / jnp.sqrt(mean + epsilon)
        parts.append(normed * gain * (gate / (1.0 + jnp.exp(-gate))))
    headout = jnp.concatenate(parts, axis=1).astype(jnp.bfloat16)
    chip, core = lax.axis_index("heads_0"), lax.axis_index("heads_1")
    first = jnp.where((chip == 0) & (core == 0), 1.0, 0.0)
    finished = []
    lines = wide // 128
    cores, halves = 2, out_ref.shape[0] // rows
    for n in range(blocks):
        copies[small + heads + n].wait()
        part = slice(n * wide, (n + 1) * wide)
        total = jnp.dot(headout, proj_ref[:, part], preferred_element_type=jnp.float32)
        total = total + res_ref[:, part].astype(jnp.float32) * first
        total = total.reshape(rows, lines, 128)
        for row in range(rows):
            for half in range(halves):
                core, r = row // (rows // cores), row % (rows // cores)
                place = (r * halves + half) * cores + core
                done_ref[place, n * lines : (n + 1) * lines, :] = total[row]
        part = pl.ds(n * lines, lines)
        finished.append(
            pltpu.make_async_copy(done_ref.at[:, part], out_ref.at[:, part], out_sems.at[n])
        )
        finished[-1].start()
    for copy in finished:
        copy.wait()


def head_partials(
    queries,
    keys_new,
    values_new,
    out_gate,
    decay_logit,
    beta_logit,
    decay_rate,
    state,
    norm_gain,
    out_proj,
    residual,
    places,
):
    arrays = (
        queries,
        keys_new,
        values_new,
        out_gate,
        decay_logit.T,
        beta_logit.T,
        norm_gain.reshape(1, -1),
        decay_rate.reshape(1, -1),
        residual,
        state,
        out_proj,
    )
    width = out_proj.shape[1]
    return pl.pallas_call(
        heads_kernel,
        out_shape=jax.ShapeDtypeStruct((places, width // 128, 128), jnp.float32),
        in_specs=[any_spec() for _ in arrays],
        out_specs=any_spec(),
        scratch_shapes=[pltpu.VMEM(a.shape, a.dtype) for a in arrays]
        + [
            pltpu.VMEM((places, width // 128, 128), jnp.float32),
            pltpu.SemaphoreType.DMA((9 + state.shape[1] + 4,)),
            pltpu.SemaphoreType.DMA((4,)),
        ],
        cost_estimate=pl.CostEstimate(flops=40000000, bytes_accessed=3500000, transcendentals=0),
        name="heads",
    )(*arrays)


def norm_kernel(half_ref, arrived_ref, gain_ref, weight_ref, piece_ref, value_ref, scratch):
    width = gain_ref.size
    hsum = arrived_ref[0]
    for n in range(1, arrived_ref.shape[0]):
        hsum = hsum + arrived_ref[n]
    gain = gain_ref[...]
    squares = jnp.sum(hsum * hsum, axis=(0, 1), keepdims=True)
    terms = jnp.sum(hsum * gain * weight_ref[...], axis=(0, 1), keepdims=True)
    rstd = 1.0 / jnp.sqrt(squares / width + epsilon)
    scratch[...] = hsum * rstd * gain
    lines = piece_ref.shape[1]
    start = pl.multiple_of(half_ref[0] * lines, lines)
    piece = scratch[pl.ds(start, lines), :].astype(jnp.bfloat16)
    for n in range(piece_ref.shape[0]):
        piece_ref[n] = piece
    value_ref[...] = jnp.broadcast_to(rstd * terms, value_ref.shape)


def norm_pieces(arrived, gain, weight, half, copies, lines):
    return pl.pallas_call(
        norm_kernel,
        out_shape=(
            pltpu.VMEM((copies, lines, 128), jnp.bfloat16),
            pltpu.VMEM((1, 128), jnp.float32),
        ),
        in_specs=[smem_spec(), vmem_spec(), vmem_spec(), vmem_spec()],
        out_specs=(vmem_spec(), vmem_spec()),
        scratch_shapes=[pltpu.VMEM(gain.shape, jnp.float32)],
        cost_estimate=pl.CostEstimate(flops=4000000, bytes_accessed=400000, transcendentals=0),
        compiler_params=room(4),
        name="norm",
    )(half, arrived, gain, weight)


def logits_kernel(groups, near_ref, far_ref, ids_ref, *refs):
    count = 4
    matrices, out_ref, local, rows, flat, sems = refs[:count], *refs[count:]
    tiles, lanes = near_ref.shape[1:]
    pieces = flat.shape[0] // (groups * tiles)
    deep = tiles * lanes
    halves = local.shape[0] // deep
    pair, core, side = (lax.axis_index(a) for a in ("x_pair", "heads_1", "x_side"))
    flat_place = 0
    for axis in HEADS_BATCH:
        flat_place = flat_place * lax.axis_size(axis) + lax.axis_index(axis)
    across = (1 - 2 * core) * lax.axis_size(BATCH)
    along = (1 - 2 * side) * lax.axis_size("x_pair")
    firsts = [(flat_place + step) * lanes for step in (0, across, along, across + along)]
    moved = [
        pltpu.make_async_copy(near_ref, rows.at[pair], sems.at[halves]),
        pltpu.make_async_copy(far_ref, rows.at[1 - pair], sems.at[halves + 1]),
    ]
    for copy in moved:
        copy.start()
    copies = []
    for k in range(halves):
        part = pl.ds(k * deep, deep)
        copies.append(
            pltpu.make_async_copy(matrices[-1].at[part], local.at[part], sems.at[k])
        )
    for copy in copies:
        copy.start()
    for copy in moved:
        copy.wait()
    flat[...] = rows[...].reshape(flat.shape).astype(jnp.float32)

    def rows_of(piece):
        first, step = piece * tiles, pieces * tiles
        return jnp.concatenate(
            [flat[pl.ds(first + t, groups, stride=step), :] for t in range(tiles)], axis=1
        ).astype(jnp.bfloat16)

    sums = [None] * count
    for k in range(halves):
        part = slice(k * deep, (k + 1) * deep)
        lhs = jnp.concatenate([rows_of(p) for p in range(k, pieces, halves)], axis=0)
        for n in range(count):
            if n == count - 1:
                copies[k].wait()
            matrix = matrices[n] if n < count - 1 else local
            term = jnp.dot(lhs, matrix[part, :], preferred_element_type=jnp.float32)
            sums[n] = term if k == 0 else sums[n] + term
    top = sums[0]
    for n in range(1, count):
        top = jnp.maximum(top, sums[n])
    top = jnp.max(top, axis=1, keepdims=True)
    ids = ids_ref[...]
    total = jnp.zeros(sums[0].shape, jnp.float32)
    chosen = jnp.zeros(sums[0].shape, jnp.float32)
    for n in range(count):
        total = total + jnp.exp(sums[n] - top)
        columns = lax.broadcasted_iota(jnp.int32, sums[n].shape, 1) + firsts[n]
        chosen = chosen + jnp.where(columns == ids, sums[n], 0.0)
    total = jnp.sum(total, axis=1, keepdims=True)
    chosen = jnp.sum(chosen, axis=1, keepdims=True)
    lane = lax.broadcasted_iota(jnp.int32, (groups, 128), 1)
    packed = jnp.zeros((groups, 128), jnp.float32)
    owned = pieces // halves
    for n, column in enumerate((top, total, chosen)):
        for r in range(owned):
            part = column[r * groups : (r + 1) * groups]
            packed = jnp.where(lane == n * owned + r, part, packed)
    for g in range(groups):
        out_ref[g] = packed[g : g + 1]


def logit_stats(near_rows, far_rows, matrices, ids, groups):
    depth = matrices[0].shape[0]
    return pl.pallas_call(
        functools.partial(logits_kernel, groups),
        out_shape=pltpu.VMEM((groups, 1, 128), jnp.float32),
        in_specs=[any_spec(), any_spec(), vmem_spec()]
        + [vmem_spec() for _ in matrices[:-1]]
        + [any_spec()],
        out_specs=vmem_spec(),
        scratch_shapes=[
            pltpu.VMEM((depth, 128), jnp.bfloat16),
            pltpu.VMEM((2, *near_rows.shape), near_rows.dtype),
            pltpu.VMEM((2 * near_rows.size // 128, 128), jnp.float32),
            pltpu.SemaphoreType.DMA((4,)),
        ],
        cost_estimate=pl.CostEstimate(flops=270000000, bytes_accessed=4700000, transcendentals=0),
        compiler_params=room(12),
        name="logits",
    )(near_rows, far_rows, ids, *matrices)


def shifted(lines, places):
    return pltpu.roll(lines, places % 128, 1)


def merged(lines, keep, owned):
    low = jnp.min(lines, axis=0, keepdims=True)
    top = jnp.max(jnp.where(keep, lines, low), axis=0, keepdims=True)
    weight = jnp.where(keep, jnp.exp(jnp.minimum(lines - top, 0.0)), 0.0)
    total = jnp.sum(shifted(lines, -owned) * weight, axis=0, keepdims=True)
    chosen = jnp.sum(jnp.where(keep, lines, 0.0), axis=0, keepdims=True)
    return top, total, chosen


def group_kernel(owned, stats_ref, value_ref, out_ref):
    lines = stats_ref[...].reshape(stats_ref.shape[0], 128)
    top, total, chosen = merged(lines, jnp.full(lines.shape, True), owned)
    lane = lax.broadcasted_iota(jnp.int32, (1, 128), 1)
    packed = jnp.where(lane < owned, top, shifted(total, owned))
    packed = jnp.where(lane < 2 * owned, packed, chosen)
    packed = jnp.where(lane < 3 * owned, packed, value_ref[...])
    for n in range(out_ref.shape[0]):
        out_ref[n] = packed


def group_stats(stats, value, owned, copies):
    return pl.pallas_call(
        functools.partial(group_kernel, owned),
        out_shape=pltpu.VMEM((copies, 1, 128), jnp.float32),
        in_specs=[vmem_spec(), vmem_spec()],
        out_specs=vmem_spec(),
        compiler_params=room(2),
        name="group",
    )(stats, value)


def final_kernel(owned, cores, stats_ref, logprob_ref, value_ref):
    count = stats_ref.shape[0]
    lines = stats_ref[...].reshape(count, 128)
    place = lax.broadcasted_iota(jnp.int32, lines.shape, 0)
    lane = lax.broadcasted_iota(jnp.int32, lines.shape, 1)
    row = lax.broadcasted_iota(jnp.int32, (1, 128), 1)
    logprob = jnp.zeros((1, 128), jnp.float32)
    for core in range(cores):
        top, total, chosen = merged(lines, place % cores == core, owned)
        total = jnp.where(row < owned, total, 1.0)
        found = shifted(chosen, -2 * owned) - (top + jnp.log(total))
        logprob = jnp.where(row // owned == core, shifted(found, core * owned), logprob)
    values = jnp.broadcast_to(lines[:, 3 * owned : 3 * owned + 1], lines.shape)
    here = place == (lane % owned) * (count // owned) + lane // owned
    value = jnp.sum(jnp.where(here, values, 0.0), axis=0, keepdims=True)
    logprob_ref[...] = logprob[:, : logprob_ref.shape[1]]
    value_ref[...] = value[:, : value_ref.shape[1]]


def final_values(stats, owned, cores):
    rows = owned * cores
    return pl.pallas_call(
        functools.partial(final_kernel, owned, cores),
        out_shape=(
            jax.ShapeDtypeStruct((1, rows), jnp.float32),
            jax.ShapeDtypeStruct((1, rows), jnp.float32),
        ),
        in_specs=[vmem_spec()],
        out_specs=(vmem_spec(), vmem_spec()),
        compiler_params=room(2),
        name="final",
    )(stats)


def per_device(
    queries,
    keys_new,
    values_new,
    out_gate,
    decay_logit,
    beta_logit,
    decay_rate,
    state,
    norm_gain,
    out_proj,
    residual,
    final_gain,
    value_weight,
    lm_head,
    sampled,
):
    chips, cores = lax.axis_size("heads_0"), lax.axis_size("heads_1")
    groups = lax.axis_size(GROUP)
    chip, core = lax.axis_index("heads_0"), lax.axis_index("heads_1")
    side = lax.axis_index("x_side")
    rows_own, width = residual.shape
    rows_core = rows_own // cores
    copies = chips // rows_core
    lanes = 128
    lines = width // lanes

    x_head = lax.ppermute(lm_head, "x_side", SWAP)
    core_head = lax.ppermute(lm_head, "heads_1", SWAP)
    both_head = lax.ppermute(x_head, "heads_1", SWAP)
    partial_out = head_partials(
        queries,
        keys_new,
        values_new,
        out_gate,
        decay_logit,
        beta_logit,
        decay_rate,
        state,
        norm_gain,
        out_proj,
        residual,
        chips * cores,
    )
    arrived = exchange(partial_out, HEADS)
    gain = final_gain.reshape(lines, lanes)
    weight = value_weight.reshape(lines, lanes)
    half_here = (chip % copies).astype(jnp.int32).reshape(1)
    near = lax.axis_size(NEAR)
    pieces, value = norm_pieces(arrived, gain, weight, half_here, near, lines // copies)
    near_rows = exchange(pieces, NEAR)
    far_rows = lax.ppermute(near_rows, "x_pair", SWAP)

    matrices = (lm_head, core_head, x_head, both_head)
    ids = sampled.reshape(lax.axis_size("z"), lax.axis_size("x_side"), -1, cores, rows_core)
    ids = lax.dynamic_index_in_dim(ids, side, 1, keepdims=False)
    ids = lax.dynamic_index_in_dim(ids, core, 2, keepdims=False)
    ids = ids.transpose(2, 1, 0).reshape(-1, 1)
    stats = logit_stats(near_rows, far_rows, matrices, ids, groups)
    stats = group_stats(exchange(stats, GROUP), value, rows_core, chips * cores)
    logprob, values = final_values(exchange(stats, HEADS), rows_core, cores)
    return (logprob.reshape(-1), values.reshape(-1))


def solution(mesh):
    torus = Mesh(
        mesh.devices.reshape(8, 2, 8, 2, 2), ("heads_0", "heads_1", "z", "x_side", "x_pair")
    )
    return jax.shard_map(
        per_device,
        mesh=torus,
        in_specs=(
            P(BATCH, HEADS),
            P(BATCH, HEADS),
            P(BATCH, HEADS),
            P(BATCH, HEADS),
            P(BATCH, HEADS),
            P(BATCH, HEADS),
            P(HEADS),
            P(BATCH, HEADS, None, None),
            P(),
            P(HEADS, None),
            P(BATCH, None),
            P(),
            P(),
            P(None, HEADS_BATCH),
            P(),
        ),
        out_specs=(P(BATCH), P(BATCH)),
        check_vma=False,
    )
```

profile of v0, /device:TPU:1, one launch (start us, length us, event | category | flops | bytes accessed | tf_op | source)
XLA Modules:
  0.0 99.5 jit_solution(5277522207976371783)
XLA Ops:
  0.6 0.0 copy-start
  0.6 0.0 copy-start.2
  0.7 0.0 copy-start.1
  0.7 5.6 %collective-permute-start.2 = (bf16[4096,128]{1,0:T(8,128)(2,1)}, bf16[4096,128]{1,0:T(8,128)(2,1)S(1)}, u32[]{:S(2)}, u32[]{:S(2)}) collective-permute-start(bf16[4096,128]{1,0:T(8,128)(2,1)} %refs_0_.3), channel_id=1, source_target_pairs={{0,2},{2,0},{1,3},{3,1},{4,6},{6,4},{5,7},{7,5},{8,10},{10,8},{9,1... | collective-permute-start | bytes 3145736 | tf_op jit(solution)/shard_map/ppermute | solution.py:407
  6.3 0.0 copy-start.3
  6.3 3.8 %heads.1 = f32[16,32,128]{2,1,0:T(8,128)} custom-call(bf16[8,256]{1,0:T(8,128)(2,1)} %refs_0_.2, bf16[8,256]{1,0:T(8,128)(2,1)} %refs_1_.1, bf16[8,256]{1,0:T(8,128)(2,1)} %refs_2_.1, bf16[8,256]{1,0:T(8,128)(2,1)} %refs_3_.1, f32[2,8]{1,0:T(2,128)} %bitcast.15, f32[2,8]{1,0:T(2,128)} %bitcast.16, f32[1,128]{1,0:T(1,128)} %bitcast.17, f32[1,2]{1,0:T(1,128)} %bitcast.18, ...), custom_call_target="tpu_custom_call" | custom-call | flops 40000000 | bytes 3500000 | tf_op jit(solution)/shard_map/heads/pallas_call | solution.py:168
  10.1 8.1 %all-to-all-start = ((f32[16,32,128]{2,1,0:T(8,128)}), f32[16,32,128]{2,1,0:T(8,128)S(1)}, u32[]{:S(2)}, u32[]{:S(2)}) async-start(f32[16,32,128]{2,1,0:T(8,128)} %heads.1), calls=%async_computation | async-start | bytes 524288 | tf_op jit(solution)/shard_map/all_to_all | solution.py:24
  18.2 0.0 copy-done
  18.2 2.0 %collective-permute-start.1 = (bf16[4096,128]{1,0:T(8,128)(2,1)S(1)}, bf16[4096,128]{1,0:T(8,128)(2,1)S(1)}, u32[]{:S(2)}, u32[]{:S(2)}) collective-permute-start(bf16[4096,128]{1,0:T(8,128)(2,1)S(1)} %copy-done), channel_id=1, source_target_pairs={{0,32},{32,0},{1,33},{33,1},{2,34},{34,2},{3,35},{35,3},{4,36},{36... | collective-permute-start | bytes 3145736 | tf_op jit(solution)/shard_map/ppermute | solution.py:408
  20.2 5.9 %collective-permute-done.2.refs_2_ = bf16[4096,128]{1,0:T(8,128)(2,1)S(1)} collective-permute-done((bf16[4096,128]{1,0:T(8,128)(2,1)}, bf16[4096,128]{1,0:T(8,128)(2,1)S(1)}, u32[]{:S(2)}, u32[]{:S(2)}) %collective-permute-start.2) | collective-permute-done | bytes 1048608 | tf_op jit(solution)/shard_map/ppermute | solution.py:407
  26.1 6.4 %collective-permute-start.3 = (bf16[4096,128]{1,0:T(8,128)(2,1)S(1)}, bf16[4096,128]{1,0:T(8,128)(2,1)}, u32[]{:S(2)}, u32[]{:S(2)}) collective-permute-start(bf16[4096,128]{1,0:T(8,128)(2,1)S(1)} %collective-permute-done.2.refs_2_), channel_id=1, source_target_pairs={{0,32},{32,0},{1,33},{33,1},{2,34},{34,2},{3,35},{35,3},{4,36},{36... | collective-permute-start | bytes 3145736 | tf_op jit(solution)/shard_map/ppermute | solution.py:409
  32.5 0.0 all-to-all-done.arrived_ref
  32.5 0.0 copy-done.2
  32.5 0.0 copy-done.1
  32.5 0.2 norm.1
  32.7 29.9 %all_to_all.20.near_ref = bf16[64,16,128]{2,1,0:T(8,128)(2,1)S(1)} all-to-all(bf16[64,16,128]{2,1,0:T(8,128)(2,1)S(1)} %get-tuple-element.6), channel_id=1, replica_groups=mesh['heads_0'=8,'heads_1'=2,'z'=8,'x_side'=2,'x_pair'=2] {'z','heads_0'}, dimensions={0} | all-to-all | bytes 524288 | tf_op jit(solution)/shard_map/all_to_all | solution.py:24
  62.6 3.1 %collective-permute-start = (bf16[64,16,128]{2,1,0:T(8,128)(2,1)S(1)}, bf16[64,16,128]{2,1,0:T(8,128)(2,1)}, u32[]{:S(2)}, u32[]{:S(2)}) collective-permute-start(bf16[64,16,128]{2,1,0:T(8,128)(2,1)S(1)} %all_to_all.20.near_ref), channel_id=1, source_target_pairs={{0,1},{1,0},{2,3},{3,2},{4,5},{5,4},{6,7},{7,6},{8,9},{9,8},{10,11... | collective-permute-start | bytes 786440 | tf_op jit(solution)/shard_map/ppermute | solution.py:431
  65.7 0.0 copy-done.3
  65.8 0.1 reshape.38
  65.9 0.1 copy.19
  66.0 0.1 reshape.42.ids_ref
  66.1 0.0 collective-permute-done.1.refs_1_
  66.1 4.2 %collective-permute-done.far_ref = bf16[64,16,128]{2,1,0:T(8,128)(2,1)} collective-permute-done((bf16[64,16,128]{2,1,0:T(8,128)(2,1)S(1)}, bf16[64,16,128]{2,1,0:T(8,128)(2,1)}, u32[]{:S(2)}, u32[]{:S(2)}) %collective-permute-start) | collective-permute-done | bytes 262176 | tf_op jit(solution)/shard_map/ppermute | solution.py:431
  70.2 0.0 collective-permute-done.3.refs_3_
  70.2 2.9 %logits.1 = f32[16,1,128]{2,1,0:T(1,128)S(1)} custom-call(bf16[64,16,128]{2,1,0:T(8,128)(2,1)S(1)} %all_to_all.20.near_ref, bf16[64,16,128]{2,1,0:T(8,128)(2,1)} %collective-permute-done.far_ref, s32[64,1]{1,0:T(8,128)S(1)} %reshape.42.ids_ref, bf16[4096,128]{1,0:T(8,128)(2,1)S(1)} %copy-done, bf16[4096,128]{1,0:T(8,128)(2,1)S(1)} %collective-permute-done.1.refs_1_, ...), custom_call_target="tpu_custom_call" | custom-call | flops 270000000 | bytes 4700000 | tf_op jit(solution)/shard_map/logits/pallas_call | solution.py:292
  73.2 12.3 %all_to_all.21.stats_ref = f32[16,1,128]{2,1,0:T(1,128)S(1)} all-to-all(f32[16,1,128]{2,1,0:T(1,128)S(1)} %logits.1), channel_id=1, replica_groups=mesh['heads_0'=8,'heads_1'=2,'z'=8,'x_side'=2,'x_pair'=2] {'x_pair','z'}, dimensions={0} | all-to-all | bytes 16384 | tf_op jit(solution)/shard_map/all_to_all | solution.py:24
  85.5 0.2 group.1
  85.6 13.2 %all_to_all.22.stats_ref = f32[16,1,128]{2,1,0:T(1,128)S(1)} all-to-all(f32[16,1,128]{2,1,0:T(1,128)S(1)} %group.1), channel_id=1, replica_groups=mesh['heads_0'=8,'heads_1'=2,'z'=8,'x_side'=2,'x_pair'=2] {'heads_0','he..., dimensions={0} | all-to-all | bytes 16384 | tf_op jit(solution)/shard_map/all_to_all | solution.py:24
  98.9 0.7 final.1
  (2 shorter events, 0.0 us)
Async XLA Ops:
  0.6 17.5 %copy-start = (bf16[4096,128]{1,0:T(8,128)(2,1)S(1)}, bf16[4096,128]{1,0:T(8,128)(2,1)}, u32[]{:S(2)}) copy-start(bf16[4096,128]{1,0:T(8,128)(2,1)} %refs_0_.3) | copy-start | bytes 3145732
  0.6 31.9 %copy-start.2 = (f32[4096]{0:T(1024)S(1)}, f32[4096]{0:T(1024)}, u32[]{:S(2)}) copy-start(f32[4096]{0:T(1024)} %param.27) | copy-start | bytes 49156
  0.7 31.9 %copy-start.1 = (f32[4096]{0:T(1024)S(1)}, f32[4096]{0:T(1024)}, u32[]{:S(2)}) copy-start(f32[4096]{0:T(1024)} %param.26) | copy-start | bytes 49156
  0.7 25.4 %collective-permute-start.2 = (bf16[4096,128]{1,0:T(8,128)(2,1)}, bf16[4096,128]{1,0:T(8,128)(2,1)S(1)}, u32[]{:S(2)}, u32[]{:S(2)}) collective-permute-start(bf16[4096,128]{1,0:T(8,128)(2,1)} %refs_0_.3), channel_id=1, source_target_pairs={{0,2},{2,0},{1,3},{3,1},{4,6},{6,4},{5,7},{7,5},{8,10},{10,8},{9,1... | collective-permute-start | bytes 3145736 | tf_op jit(solution)/shard_map/ppermute | solution.py:407
  6.3 59.5 %copy-start.3 = (s32[256]{0:T(256)S(1)}, s32[256]{0:T(256)}, u32[]{:S(2)}) copy-start(s32[256]{0:T(256)} %param.29) | copy-start | bytes 3076
  10.1 22.4 %all-to-all-start = ((f32[16,32,128]{2,1,0:T(8,128)}), f32[16,32,128]{2,1,0:T(8,128)S(1)}, u32[]{:S(2)}, u32[]{:S(2)}) async-start(f32[16,32,128]{2,1,0:T(8,128)} %heads.1), calls=%async_computation | async-start | bytes 524288 | tf_op jit(solution)/shard_map/all_to_all | solution.py:24
  18.2 47.9 %collective-permute-start.1 = (bf16[4096,128]{1,0:T(8,128)(2,1)S(1)}, bf16[4096,128]{1,0:T(8,128)(2,1)S(1)}, u32[]{:S(2)}, u32[]{:S(2)}) collective-permute-start(bf16[4096,128]{1,0:T(8,128)(2,1)S(1)} %copy-done), channel_id=1, source_target_pairs={{0,32},{32,0},{1,33},{33,1},{2,34},{34,2},{3,35},{35,3},{4,36},{36... | collective-permute-start | bytes 3145736 | tf_op jit(solution)/shard_map/ppermute | solution.py:408
  26.1 44.2 %collective-permute-start.3 = (bf16[4096,128]{1,0:T(8,128)(2,1)S(1)}, bf16[4096,128]{1,0:T(8,128)(2,1)}, u32[]{:S(2)}, u32[]{:S(2)}) collective-permute-start(bf16[4096,128]{1,0:T(8,128)(2,1)S(1)} %collective-permute-done.2.refs_2_), channel_id=1, source_target_pairs={{0,32},{32,0},{1,33},{33,1},{2,34},{34,2},{3,35},{35,3},{4,36},{36... | collective-permute-start | bytes 3145736 | tf_op jit(solution)/shard_map/ppermute | solution.py:409
  62.6 7.6 %collective-permute-start = (bf16[64,16,128]{2,1,0:T(8,128)(2,1)S(1)}, bf16[64,16,128]{2,1,0:T(8,128)(2,1)}, u32[]{:S(2)}, u32[]{:S(2)}) collective-permute-start(bf16[64,16,128]{2,1,0:T(8,128)(2,1)S(1)} %all_to_all.20.near_ref), channel_id=1, source_target_pairs={{0,1},{1,0},{2,3},{3,2},{4,5},{5,4},{6,7},{7,6},{8,9},{9,8},{10,11... | collective-permute-start | bytes 786440 | tf_op jit(solution)/shard_map/ppermute | solution.py:431
where the time goes:
time: 100 us; the launch traced here: 99.5 us
  blocking collectives  55.4 us (55%)
  starting transfers between devices  25.2 us (25%)
  waiting for transfers between devices  10 us (10%)
  Pallas kernels  7.72 us (8%)
    all_to_all x3, blocking collectives, exchange(): return lax.all_to_all(parts, axis, split_axis=0, concat_axis=0, tiled=True)  55.4 us
    all_to_all x1, starting transfers between devices, exchange(): return lax.all_to_all(parts, axis, split_axis=0, concat_axis=0, tiled=True)  8.08 us
    ppermute x1, starting transfers between devices, per_device(): both_head = lax.ppermute(x_head, 'heads_1', SWAP)  6.41 us
    ppermute x1, waiting for transfers between devices, per_device(): x_head = lax.ppermute(lm_head, 'x_side', SWAP)  5.89 us
    ppermute x1, starting transfers between devices, per_device(): x_head = lax.ppermute(lm_head, 'x_side', SWAP)  5.6 us
    ppermute x1, waiting for transfers between devices, per_device(): far_rows = lax.ppermute(near_rows, 'x_pair', SWAP)  4.15 us
    pallas_call x1, Pallas kernels, head_partials(): pl.pallas_call(heads_kernel, out_shape=jax.ShapeDtypeStruct((places, widt...  3.79 us
    ppermute x1, starting transfers between devices, per_device(): far_rows = lax.ppermute(near_rows, 'x_pair', SWAP)  3.11 us
  transfers between devices with their start and end apart: 5, of which 2 were waited for; matrix products, arithmetic and copies ran while one was open for 0% of the time, Pallas kernels for 4%

commit v1 on v0

--- a/solution.py
+++ b/solution.py
@@ -12,7 +12,7 @@
 HEADS = ("heads_0", "heads_1")
 BATCH = ("z", "x_side", "x_pair")
 GROUP = ("x_pair", "z")
-NEAR = ("z", "heads_0")
+NEAR = ("heads_0", "z")
 HEADS_BATCH = ("heads_0", "heads_1", "z", "x_side", "x_pair")
 SWAP = [(0, 1), (1, 0)]
 
@@ -248,10 +248,15 @@
     flat[...] = rows[...].reshape(flat.shape).astype(jnp.float32)
 
     def rows_of(piece):
-        first, step = piece * tiles, pieces * tiles
-        return jnp.concatenate(
-            [flat[pl.ds(first + t, groups, stride=step), :] for t in range(tiles)], axis=1
-        ).astype(jnp.bfloat16)
+        each = groups // 2
+        lines = []
+        for t in range(tiles):
+            at = piece * each * tiles + t
+            found = [
+                flat[pl.ds(at + n * pieces * each * tiles, each, stride=tiles), :] for n in range(2)
+            ]
+            lines.append(jnp.concatenate(found, axis=0))
+        return jnp.concatenate(lines, axis=1).astype(jnp.bfloat16)
 
     sums = [None] * count
     for k in range(halves):

time: 100 us -> 100 us (level)
  no operation moved by 1% of the time
where the time goes in v1:
time: 100 us; the launch traced here: 99.5 us
  blocking collectives  55.7 us (56%)
  starting transfers between devices  25.2 us (25%)
  waiting for transfers between devices  10.1 us (10%)
  Pallas kernels  7.43 us (7%)
    all_to_all x3, blocking collectives, exchange(): return lax.all_to_all(parts, axis, split_axis=0, concat_axis=0, tiled=True)  55.7 us
    all_to_all x1, starting transfers between devices, exchange(): return lax.all_to_all(parts, axis, split_axis=0, concat_axis=0, tiled=True)  8.08 us
    ppermute x1, starting transfers between devices, per_device(): both_head = lax.ppermute(x_head, 'heads_1', SWAP)  6.41 us
    ppermute x1, waiting for transfers between devices, per_device(): x_head = lax.ppermute(lm_head, 'x_side', SWAP)  5.89 us
    ppermute x1, starting transfers between devices, per_device(): x_head = lax.ppermute(lm_head, 'x_side', SWAP)  5.6 us
    ppermute x1, waiting for transfers between devices, per_device(): far_rows = lax.ppermute(near_rows, 'x_pair', SWAP)  4.17 us
    pallas_call x1, Pallas kernels, head_partials(): pl.pallas_call(heads_kernel, out_shape=jax.ShapeDtypeStruct((places, widt...  3.79 us
    ppermute x1, starting transfers between devices, per_device(): far_rows = lax.ppermute(near_rows, 'x_pair', SWAP)  3.11 us
  transfers between devices with their start and end apart: 5, of which 2 were waited for; matrix products, arithmetic and copies ran while one was open for 0% of the time, Pallas kernels for 4%

profile of v1, /device:TPU:1, one launch (start us, length us, event | category | flops | bytes accessed | tf_op | source)
XLA Modules:
  0.0 99.5 jit_solution(5469100603790884477)
XLA Ops:
  0.6 0.0 copy-start
  0.6 0.0 copy-start.2
  0.7 0.0 copy-start.1
  0.7 5.6 %collective-permute-start.2 = (bf16[4096,128]{1,0:T(8,128)(2,1)}, bf16[4096,128]{1,0:T(8,128)(2,1)S(1)}, u32[]{:S(2)}, u32[]{:S(2)}) collective-permute-start(bf16[4096,128]{1,0:T(8,128)(2,1)} %refs_0_.3), channel_id=1, source_target_pairs={{0,2},{2,0},{1,3},{3,1},{4,6},{6,4},{5,7},{7,5},{8,10},{10,8},{9,1... | collective-permute-start | bytes 3145736 | tf_op jit(solution)/shard_map/ppermute | solution.py:412
  6.3 0.0 copy-start.3
  6.3 3.8 %heads.1 = f32[16,32,128]{2,1,0:T(8,128)} custom-call(bf16[8,256]{1,0:T(8,128)(2,1)} %refs_0_.2, bf16[8,256]{1,0:T(8,128)(2,1)} %refs_1_.1, bf16[8,256]{1,0:T(8,128)(2,1)} %refs_2_.1, bf16[8,256]{1,0:T(8,128)(2,1)} %refs_3_.1, f32[2,8]{1,0:T(2,128)} %bitcast.15, f32[2,8]{1,0:T(2,128)} %bitcast.16, f32[1,128]{1,0:T(1,128)} %bitcast.17, f32[1,2]{1,0:T(1,128)} %bitcast.18, ...), custom_call_target="tpu_custom_call" | custom-call | flops 40000000 | bytes 3500000 | tf_op jit(solution)/shard_map/heads/pallas_call | solution.py:168
  10.1 8.1 %all-to-all-start = ((f32[16,32,128]{2,1,0:T(8,128)}), f32[16,32,128]{2,1,0:T(8,128)S(1)}, u32[]{:S(2)}, u32[]{:S(2)}) async-start(f32[16,32,128]{2,1,0:T(8,128)} %heads.1), calls=%async_computation | async-start | bytes 524288 | tf_op jit(solution)/shard_map/all_to_all | solution.py:24
  18.2 0.0 copy-done
  18.2 2.0 %collective-permute-start.1 = (bf16[4096,128]{1,0:T(8,128)(2,1)S(1)}, bf16[4096,128]{1,0:T(8,128)(2,1)S(1)}, u32[]{:S(2)}, u32[]{:S(2)}) collective-permute-start(bf16[4096,128]{1,0:T(8,128)(2,1)S(1)} %copy-done), channel_id=1, source_target_pairs={{0,32},{32,0},{1,33},{33,1},{2,34},{34,2},{3,35},{35,3},{4,36},{36... | collective-permute-start | bytes 3145736 | tf_op jit(solution)/shard_map/ppermute | solution.py:413
  20.2 5.9 %collective-permute-done.2.refs_2_ = bf16[4096,128]{1,0:T(8,128)(2,1)S(1)} collective-permute-done((bf16[4096,128]{1,0:T(8,128)(2,1)}, bf16[4096,128]{1,0:T(8,128)(2,1)S(1)}, u32[]{:S(2)}, u32[]{:S(2)}) %collective-permute-start.2) | collective-permute-done | bytes 1048608 | tf_op jit(solution)/shard_map/ppermute | solution.py:412
  26.1 6.4 %collective-permute-start.3 = (bf16[4096,128]{1,0:T(8,128)(2,1)S(1)}, bf16[4096,128]{1,0:T(8,128)(2,1)}, u32[]{:S(2)}, u32[]{:S(2)}) collective-permute-start(bf16[4096,128]{1,0:T(8,128)(2,1)S(1)} %collective-permute-done.2.refs_2_), channel_id=1, source_target_pairs={{0,32},{32,0},{1,33},{33,1},{2,34},{34,2},{3,35},{35,3},{4,36},{36... | collective-permute-start | bytes 3145736 | tf_op jit(solution)/shard_map/ppermute | solution.py:414
  32.5 0.0 all-to-all-done.arrived_ref
  32.5 0.0 copy-done.2
  32.5 0.0 copy-done.1
  32.5 0.2 norm.1
  32.7 29.8 %all_to_all.20.near_ref = bf16[64,16,128]{2,1,0:T(8,128)(2,1)S(1)} all-to-all(bf16[64,16,128]{2,1,0:T(8,128)(2,1)S(1)} %get-tuple-element.6), channel_id=1, replica_groups=mesh['heads_0'=8,'heads_1'=2,'z'=8,'x_side'=2,'x_pair'=2] {'heads_0','z'}, dimensions={0} | all-to-all | bytes 524288 | tf_op jit(solution)/shard_map/all_to_all | solution.py:24
  62.5 3.1 %collective-permute-start = (bf16[64,16,128]{2,1,0:T(8,128)(2,1)S(1)}, bf16[64,16,128]{2,1,0:T(8,128)(2,1)}, u32[]{:S(2)}, u32[]{:S(2)}) collective-permute-start(bf16[64,16,128]{2,1,0:T(8,128)(2,1)S(1)} %all_to_all.20.near_ref), channel_id=1, source_target_pairs={{0,1},{1,0},{2,3},{3,2},{4,5},{5,4},{6,7},{7,6},{8,9},{9,8},{10,11... | collective-permute-start | bytes 786440 | tf_op jit(solution)/shard_map/ppermute | solution.py:436
  65.6 0.0 copy-done.3
  65.6 0.1 reshape.38
  65.8 0.1 copy.19
  65.9 0.1 reshape.42.ids_ref
  66.0 0.0 collective-permute-done.1.refs_1_
  66.0 4.2 %collective-permute-done.far_ref = bf16[64,16,128]{2,1,0:T(8,128)(2,1)} collective-permute-done((bf16[64,16,128]{2,1,0:T(8,128)(2,1)S(1)}, bf16[64,16,128]{2,1,0:T(8,128)(2,1)}, u32[]{:S(2)}, u32[]{:S(2)}) %collective-permute-start) | collective-permute-done | bytes 262176 | tf_op jit(solution)/shard_map/ppermute | solution.py:436
  70.2 0.0 collective-permute-done.3.refs_3_
  70.2 2.6 %logits.1 = f32[16,1,128]{2,1,0:T(1,128)S(1)} custom-call(bf16[64,16,128]{2,1,0:T(8,128)(2,1)S(1)} %all_to_all.20.near_ref, bf16[64,16,128]{2,1,0:T(8,128)(2,1)} %collective-permute-done.far_ref, s32[64,1]{1,0:T(8,128)S(1)} %reshape.42.ids_ref, bf16[4096,128]{1,0:T(8,128)(2,1)S(1)} %copy-done, bf16[4096,128]{1,0:T(8,128)(2,1)S(1)} %collective-permute-done.1.refs_1_, ...), custom_call_target="tpu_custom_call" | custom-call | flops 270000000 | bytes 4700000 | tf_op jit(solution)/shard_map/logits/pallas_call | solution.py:297
  72.8 12.9 %all_to_all.21.stats_ref = f32[16,1,128]{2,1,0:T(1,128)S(1)} all-to-all(f32[16,1,128]{2,1,0:T(1,128)S(1)} %logits.1), channel_id=1, replica_groups=mesh['heads_0'=8,'heads_1'=2,'z'=8,'x_side'=2,'x_pair'=2] {'x_pair','z'}, dimensions={0} | all-to-all | bytes 16384 | tf_op jit(solution)/shard_map/all_to_all | solution.py:24
  85.7 0.2 group.1
  85.9 13.0 %all_to_all.22.stats_ref = f32[16,1,128]{2,1,0:T(1,128)S(1)} all-to-all(f32[16,1,128]{2,1,0:T(1,128)S(1)} %group.1), channel_id=1, replica_groups=mesh['heads_0'=8,'heads_1'=2,'z'=8,'x_side'=2,'x_pair'=2] {'heads_0','he..., dimensions={0} | all-to-all | bytes 16384 | tf_op jit(solution)/shard_map/all_to_all | solution.py:24
  98.9 0.7 final.1
  (2 shorter events, 0.0 us)
Async XLA Ops:
  0.6 17.5 %copy-start = (bf16[4096,128]{1,0:T(8,128)(2,1)S(1)}, bf16[4096,128]{1,0:T(8,128)(2,1)}, u32[]{:S(2)}) copy-start(bf16[4096,128]{1,0:T(8,128)(2,1)} %refs_0_.3) | copy-start | bytes 3145732
  0.6 31.9 %copy-start.2 = (f32[4096]{0:T(1024)S(1)}, f32[4096]{0:T(1024)}, u32[]{:S(2)}) copy-start(f32[4096]{0:T(1024)} %param.27) | copy-start | bytes 49156
  0.7 31.9 %copy-start.1 = (f32[4096]{0:T(1024)S(1)}, f32[4096]{0:T(1024)}, u32[]{:S(2)}) copy-start(f32[4096]{0:T(1024)} %param.26) | copy-start | bytes 49156
  0.7 25.4 %collective-permute-start.2 = (bf16[4096,128]{1,0:T(8,128)(2,1)}, bf16[4096,128]{1,0:T(8,128)(2,1)S(1)}, u32[]{:S(2)}, u32[]{:S(2)}) collective-permute-start(bf16[4096,128]{1,0:T(8,128)(2,1)} %refs_0_.3), channel_id=1, source_target_pairs={{0,2},{2,0},{1,3},{3,1},{4,6},{6,4},{5,7},{7,5},{8,10},{10,8},{9,1... | collective-permute-start | bytes 3145736 | tf_op jit(solution)/shard_map/ppermute | solution.py:412
  6.3 59.4 %copy-start.3 = (s32[256]{0:T(256)S(1)}, s32[256]{0:T(256)}, u32[]{:S(2)}) copy-start(s32[256]{0:T(256)} %param.29) | copy-start | bytes 3076
  10.1 22.4 %all-to-all-start = ((f32[16,32,128]{2,1,0:T(8,128)}), f32[16,32,128]{2,1,0:T(8,128)S(1)}, u32[]{:S(2)}, u32[]{:S(2)}) async-start(f32[16,32,128]{2,1,0:T(8,128)} %heads.1), calls=%async_computation | async-start | bytes 524288 | tf_op jit(solution)/shard_map/all_to_all | solution.py:24
  18.2 47.8 %collective-permute-start.1 = (bf16[4096,128]{1,0:T(8,128)(2,1)S(1)}, bf16[4096,128]{1,0:T(8,128)(2,1)S(1)}, u32[]{:S(2)}, u32[]{:S(2)}) collective-permute-start(bf16[4096,128]{1,0:T(8,128)(2,1)S(1)} %copy-done), channel_id=1, source_target_pairs={{0,32},{32,0},{1,33},{33,1},{2,34},{34,2},{3,35},{35,3},{4,36},{36... | collective-permute-start | bytes 3145736 | tf_op jit(solution)/shard_map/ppermute | solution.py:413
  26.1 44.1 %collective-permute-start.3 = (bf16[4096,128]{1,0:T(8,128)(2,1)S(1)}, bf16[4096,128]{1,0:T(8,128)(2,1)}, u32[]{:S(2)}, u32[]{:S(2)}) collective-permute-start(bf16[4096,128]{1,0:T(8,128)(2,1)S(1)} %collective-permute-done.2.refs_2_), channel_id=1, source_target_pairs={{0,32},{32,0},{1,33},{33,1},{2,34},{34,2},{3,35},{35,3},{4,36},{36... | collective-permute-start | bytes 3145736 | tf_op jit(solution)/shard_map/ppermute | solution.py:414
  62.5 7.6 %collective-permute-start = (bf16[64,16,128]{2,1,0:T(8,128)(2,1)S(1)}, bf16[64,16,128]{2,1,0:T(8,128)(2,1)}, u32[]{:S(2)}, u32[]{:S(2)}) collective-permute-start(bf16[64,16,128]{2,1,0:T(8,128)(2,1)S(1)} %all_to_all.20.near_ref), channel_id=1, source_target_pairs={{0,1},{1,0},{2,3},{3,2},{4,5},{5,4},{6,7},{7,6},{8,9},{9,8},{10,11... | collective-permute-start | bytes 786440 | tf_op jit(solution)/shard_map/ppermute | solution.py:436

commit v2 on v0

--- a/solution.py
+++ b/solution.py
@@ -253,16 +253,21 @@
             [flat[pl.ds(first + t, groups, stride=step), :] for t in range(tiles)], axis=1
         ).astype(jnp.bfloat16)
 
-    sums = [None] * count
-    for k in range(halves):
-        part = slice(k * deep, (k + 1) * deep)
-        lhs = jnp.concatenate([rows_of(p) for p in range(k, pieces, halves)], axis=0)
-        for n in range(count):
+    sides = [
+        jnp.concatenate([rows_of(p) for p in range(k, pieces, halves)], axis=0)
+        for k in range(halves)
+    ]
+    sums = []
+    for n in range(count):
+        term = None
+        for k in range(halves):
+            part = slice(k * deep, (k + 1) * deep)
             if n == count - 1:
                 copies[k].wait()
             matrix = matrices[n] if n < count - 1 else local
-            term = jnp.dot(lhs, matrix[part, :], preferred_element_type=jnp.float32)
-            sums[n] = term if k == 0 else sums[n] + term
+            found = jnp.dot(sides[k], matrix[part, :], preferred_element_type=jnp.float32)
+            term = found if k == 0 else term + found
+        sums.append(term)
     top = sums[0]
     for n in range(1, count):
         top = jnp.maximum(top, sums[n])

time: 100 us -> 99.8 us (level)
  no operation moved by 1% of the time
where the time goes in v2:
time: 99.8 us; the launch traced here: 99.4 us
  blocking collectives  55.4 us (56%)
  starting transfers between devices  25.2 us (25%)
  waiting for transfers between devices  10 us (10%)
  Pallas kernels  7.57 us (8%)
    all_to_all x3, blocking collectives, exchange(): return lax.all_to_all(parts, axis, split_axis=0, concat_axis=0, tiled=True)  55.4 us
    all_to_all x1, starting transfers between devices, exchange(): return lax.all_to_all(parts, axis, split_axis=0, concat_axis=0, tiled=True)  8.08 us
    ppermute x1, starting transfers between devices, per_device(): both_head = lax.ppermute(x_head, 'heads_1', SWAP)  6.41 us
    ppermute x1, waiting for transfers between devices, per_device(): x_head = lax.ppermute(lm_head, 'x_side', SWAP)  5.89 us
    ppermute x1, starting transfers between devices, per_device(): x_head = lax.ppermute(lm_head, 'x_side', SWAP)  5.6 us
    ppermute x1, waiting for transfers between devices, per_device(): far_rows = lax.ppermute(near_rows, 'x_pair', SWAP)  4.15 us
    pallas_call x1, Pallas kernels, head_partials(): pl.pallas_call(heads_kernel, out_shape=jax.ShapeDtypeStruct((places, widt...  3.79 us
    ppermute x1, starting transfers between devices, per_device(): far_rows = lax.ppermute(near_rows, 'x_pair', SWAP)  3.11 us
  transfers between devices with their start and end apart: 5, of which 2 were waited for; matrix products, arithmetic and copies ran while one was open for 0% of the time, Pallas kernels for 4%

profile of v2, /device:TPU:1, one launch (start us, length us, event | category | flops | bytes accessed | tf_op | source)
XLA Modules:
  0.0 99.4 jit_solution(16467751336869981863)
XLA Ops:
  0.6 0.0 copy-start
  0.6 0.0 copy-start.2
  0.7 0.0 copy-start.1
  0.7 5.6 %collective-permute-start.2 = (bf16[4096,128]{1,0:T(8,128)(2,1)}, bf16[4096,128]{1,0:T(8,128)(2,1)S(1)}, u32[]{:S(2)}, u32[]{:S(2)}) collective-permute-start(bf16[4096,128]{1,0:T(8,128)(2,1)} %refs_0_.3), channel_id=1, source_target_pairs={{0,2},{2,0},{1,3},{3,1},{4,6},{6,4},{5,7},{7,5},{8,10},{10,8},{9,1... | collective-permute-start | bytes 3145736 | tf_op jit(solution)/shard_map/ppermute | solution.py:412
  6.3 0.0 copy-start.3
  6.3 3.8 %heads.1 = f32[16,32,128]{2,1,0:T(8,128)} custom-call(bf16[8,256]{1,0:T(8,128)(2,1)} %refs_0_.2, bf16[8,256]{1,0:T(8,128)(2,1)} %refs_1_.1, bf16[8,256]{1,0:T(8,128)(2,1)} %refs_2_.1, bf16[8,256]{1,0:T(8,128)(2,1)} %refs_3_.1, f32[2,8]{1,0:T(2,128)} %bitcast.15, f32[2,8]{1,0:T(2,128)} %bitcast.16, f32[1,128]{1,0:T(1,128)} %bitcast.17, f32[1,2]{1,0:T(1,128)} %bitcast.18, ...), custom_call_target="tpu_custom_call" | custom-call | flops 40000000 | bytes 3500000 | tf_op jit(solution)/shard_map/heads/pallas_call | solution.py:168
  10.1 8.1 %all-to-all-start = ((f32[16,32,128]{2,1,0:T(8,128)}), f32[16,32,128]{2,1,0:T(8,128)S(1)}, u32[]{:S(2)}, u32[]{:S(2)}) async-start(f32[16,32,128]{2,1,0:T(8,128)} %heads.1), calls=%async_computation | async-start | bytes 524288 | tf_op jit(solution)/shard_map/all_to_all | solution.py:24
  18.2 0.0 copy-done
  18.2 2.0 %collective-permute-start.1 = (bf16[4096,128]{1,0:T(8,128)(2,1)S(1)}, bf16[4096,128]{1,0:T(8,128)(2,1)S(1)}, u32[]{:S(2)}, u32[]{:S(2)}) collective-permute-start(bf16[4096,128]{1,0:T(8,128)(2,1)S(1)} %copy-done), channel_id=1, source_target_pairs={{0,32},{32,0},{1,33},{33,1},{2,34},{34,2},{3,35},{35,3},{4,36},{36... | collective-permute-start | bytes 3145736 | tf_op jit(solution)/shard_map/ppermute | solution.py:413
  20.2 5.9 %collective-permute-done.2.refs_2_ = bf16[4096,128]{1,0:T(8,128)(2,1)S(1)} collective-permute-done((bf16[4096,128]{1,0:T(8,128)(2,1)}, bf16[4096,128]{1,0:T(8,128)(2,1)S(1)}, u32[]{:S(2)}, u32[]{:S(2)}) %collective-permute-start.2) | collective-permute-done | bytes 1048608 | tf_op jit(solution)/shard_map/ppermute | solution.py:412
  26.1 6.4 %collective-permute-start.3 = (bf16[4096,128]{1,0:T(8,128)(2,1)S(1)}, bf16[4096,128]{1,0:T(8,128)(2,1)}, u32[]{:S(2)}, u32[]{:S(2)}) collective-permute-start(bf16[4096,128]{1,0:T(8,128)(2,1)S(1)} %collective-permute-done.2.refs_2_), channel_id=1, source_target_pairs={{0,32},{32,0},{1,33},{33,1},{2,34},{34,2},{3,35},{35,3},{4,36},{36... | collective-permute-start | bytes 3145736 | tf_op jit(solution)/shard_map/ppermute | solution.py:414
  32.5 0.0 all-to-all-done.arrived_ref
  32.5 0.0 copy-done.2
  32.5 0.0 copy-done.1
  32.5 0.2 norm.1
  32.7 29.9 %all_to_all.20.near_ref = bf16[64,16,128]{2,1,0:T(8,128)(2,1)S(1)} all-to-all(bf16[64,16,128]{2,1,0:T(8,128)(2,1)S(1)} %get-tuple-element.6), channel_id=1, replica_groups=mesh['heads_0'=8,'heads_1'=2,'z'=8,'x_side'=2,'x_pair'=2] {'z','heads_0'}, dimensions={0} | all-to-all | bytes 524288 | tf_op jit(solution)/shard_map/all_to_all | solution.py:24
  62.6 3.1 %collective-permute-start = (bf16[64,16,128]{2,1,0:T(8,128)(2,1)S(1)}, bf16[64,16,128]{2,1,0:T(8,128)(2,1)}, u32[]{:S(2)}, u32[]{:S(2)}) collective-permute-start(bf16[64,16,128]{2,1,0:T(8,128)(2,1)S(1)} %all_to_all.20.near_ref), channel_id=1, source_target_pairs={{0,1},{1,0},{2,3},{3,2},{4,5},{5,4},{6,7},{7,6},{8,9},{9,8},{10,11... | collective-permute-start | bytes 786440 | tf_op jit(solution)/shard_map/ppermute | solution.py:436
  65.7 0.0 copy-done.3
  65.8 0.1 reshape.38
  65.9 0.1 copy.19
  66.0 0.1 reshape.42.ids_ref
  66.1 0.0 collective-permute-done.1.refs_1_
  66.1 4.2 %collective-permute-done.far_ref = bf16[64,16,128]{2,1,0:T(8,128)(2,1)} collective-permute-done((bf16[64,16,128]{2,1,0:T(8,128)(2,1)S(1)}, bf16[64,16,128]{2,1,0:T(8,128)(2,1)}, u32[]{:S(2)}, u32[]{:S(2)}) %collective-permute-start) | collective-permute-done | bytes 262176 | tf_op jit(solution)/shard_map/ppermute | solution.py:436
  70.2 0.0 collective-permute-done.3.refs_3_
  70.2 2.8 %logits.1 = f32[16,1,128]{2,1,0:T(1,128)S(1)} custom-call(bf16[64,16,128]{2,1,0:T(8,128)(2,1)S(1)} %all_to_all.20.near_ref, bf16[64,16,128]{2,1,0:T(8,128)(2,1)} %collective-permute-done.far_ref, s32[64,1]{1,0:T(8,128)S(1)} %reshape.42.ids_ref, bf16[4096,128]{1,0:T(8,128)(2,1)S(1)} %copy-done, bf16[4096,128]{1,0:T(8,128)(2,1)S(1)} %collective-permute-done.1.refs_1_, ...), custom_call_target="tpu_custom_call" | custom-call | flops 270000000 | bytes 4700000 | tf_op jit(solution)/shard_map/logits/pallas_call | solution.py:297
  73.0 12.3 %all_to_all.21.stats_ref = f32[16,1,128]{2,1,0:T(1,128)S(1)} all-to-all(f32[16,1,128]{2,1,0:T(1,128)S(1)} %logits.1), channel_id=1, replica_groups=mesh['heads_0'=8,'heads_1'=2,'z'=8,'x_side'=2,'x_pair'=2] {'x_pair','z'}, dimensions={0} | all-to-all | bytes 16384 | tf_op jit(solution)/shard_map/all_to_all | solution.py:24
  85.3 0.2 group.1
  85.5 13.2 %all_to_all.22.stats_ref = f32[16,1,128]{2,1,0:T(1,128)S(1)} all-to-all(f32[16,1,128]{2,1,0:T(1,128)S(1)} %group.1), channel_id=1, replica_groups=mesh['heads_0'=8,'heads_1'=2,'z'=8,'x_side'=2,'x_pair'=2] {'heads_0','he..., dimensions={0} | all-to-all | bytes 16384 | tf_op jit(solution)/shard_map/all_to_all | solution.py:24
  98.7 0.7 final.1
  (2 shorter events, 0.0 us)
Async XLA Ops:
  0.6 17.5 %copy-start = (bf16[4096,128]{1,0:T(8,128)(2,1)S(1)}, bf16[4096,128]{1,0:T(8,128)(2,1)}, u32[]{:S(2)}) copy-start(bf16[4096,128]{1,0:T(8,128)(2,1)} %refs_0_.3) | copy-start | bytes 3145732
  0.6 31.9 %copy-start.2 = (f32[4096]{0:T(1024)S(1)}, f32[4096]{0:T(1024)}, u32[]{:S(2)}) copy-start(f32[4096]{0:T(1024)} %param.27) | copy-start | bytes 49156
  0.7 31.9 %copy-start.1 = (f32[4096]{0:T(1024)S(1)}, f32[4096]{0:T(1024)}, u32[]{:S(2)}) copy-start(f32[4096]{0:T(1024)} %param.26) | copy-start | bytes 49156
  0.7 25.4 %collective-permute-start.2 = (bf16[4096,128]{1,0:T(8,128)(2,1)}, bf16[4096,128]{1,0:T(8,128)(2,1)S(1)}, u32[]{:S(2)}, u32[]{:S(2)}) collective-permute-start(bf16[4096,128]{1,0:T(8,128)(2,1)} %refs_0_.3), channel_id=1, source_target_pairs={{0,2},{2,0},{1,3},{3,1},{4,6},{6,4},{5,7},{7,5},{8,10},{10,8},{9,1... | collective-permute-start | bytes 3145736 | tf_op jit(solution)/shard_map/ppermute | solution.py:412
  6.3 59.5 %copy-start.3 = (s32[256]{0:T(256)S(1)}, s32[256]{0:T(256)}, u32[]{:S(2)}) copy-start(s32[256]{0:T(256)} %param.29) | copy-start | bytes 3076
  10.1 22.4 %all-to-all-start = ((f32[16,32,128]{2,1,0:T(8,128)}), f32[16,32,128]{2,1,0:T(8,128)S(1)}, u32[]{:S(2)}, u32[]{:S(2)}) async-start(f32[16,32,128]{2,1,0:T(8,128)} %heads.1), calls=%async_computation | async-start | bytes 524288 | tf_op jit(solution)/shard_map/all_to_all | solution.py:24
  18.2 47.9 %collective-permute-start.1 = (bf16[4096,128]{1,0:T(8,128)(2,1)S(1)}, bf16[4096,128]{1,0:T(8,128)(2,1)S(1)}, u32[]{:S(2)}, u32[]{:S(2)}) collective-permute-start(bf16[4096,128]{1,0:T(8,128)(2,1)S(1)} %copy-done), channel_id=1, source_target_pairs={{0,32},{32,0},{1,33},{33,1},{2,34},{34,2},{3,35},{35,3},{4,36},{36... | collective-permute-start | bytes 3145736 | tf_op jit(solution)/shard_map/ppermute | solution.py:413
  26.1 44.2 %collective-permute-start.3 = (bf16[4096,128]{1,0:T(8,128)(2,1)S(1)}, bf16[4096,128]{1,0:T(8,128)(2,1)}, u32[]{:S(2)}, u32[]{:S(2)}) collective-permute-start(bf16[4096,128]{1,0:T(8,128)(2,1)S(1)} %collective-permute-done.2.refs_2_), channel_id=1, source_target_pairs={{0,32},{32,0},{1,33},{33,1},{2,34},{34,2},{3,35},{35,3},{4,36},{36... | collective-permute-start | bytes 3145736 | tf_op jit(solution)/shard_map/ppermute | solution.py:414
  62.6 7.6 %collective-permute-start = (bf16[64,16,128]{2,1,0:T(8,128)(2,1)S(1)}, bf16[64,16,128]{2,1,0:T(8,128)(2,1)}, u32[]{:S(2)}, u32[]{:S(2)}) collective-permute-start(bf16[64,16,128]{2,1,0:T(8,128)(2,1)S(1)} %all_to_all.20.near_ref), channel_id=1, source_target_pairs={{0,1},{1,0},{2,3},{3,2},{4,5},{5,4},{6,7},{7,6},{8,9},{9,8},{10,11... | collective-permute-start | bytes 786440 | tf_op jit(solution)/shard_map/ppermute | solution.py:436
